TPU v7x, 32 devices: a whole 2x2x4 slice. The times are simulated.
32 devices in a mesh: tm: 8 (over z, y), series: 4 (over x, core).
Axes of the slice: x: 2, y: 2, z: 4, core: 2. Of those that a mesh axis runs over, the one named last changes fastest.
Arguments:
- signal: float32 [64, 262144], P('series', 'tm')
- valid_start: int32 [64], replicated, may hold values from 0 to 65535
- valid_end: int32 [64], replicated, may hold values from 196609 to 262144
Outputs:
- smooth: float32 [64, 262144], P('series', 'tm')
- slope: float32 [64, 262144], P('series', 'tm')
- covariance: float32 [64, 64], P('series')
Inputs may be any that keep to these rules, and one draw needn't show every extreme that they name: `valid_end`: end of the valid samples of each series.
All inputs are finite; a program needn't handle non-finite values.
Results may differ from a plain program's by a relative error of at most 0.00015.
Values sent between devices are 32-bit elements; how exact they have to be, the bound alone decides.
A program may use at most 64 MiB of HBM per device.

v0:
```python
import jax
import jax.numpy as jnp
from jax import lax
from jax.sharding import PartitionSpec as P

HALF = 16


def padded(cells, sides, width):
    for axis, dim in sides:
        count = lax.axis_size(axis)
        ends = count - 1
        head = lax.slice_in_dim(cells, 0, width, axis=dim)
        tail = lax.slice_in_dim(cells, cells.shape[dim] - width, cells.shape[dim], axis=dim)
        cells = jnp.concatenate(
            [
                lax.ppermute(tail, axis, [(i, (i + 1) % count) for i in range(ends)]),
                cells,
                lax.ppermute(head, axis, [((i + 1) % count, i) for i in range(ends)]),
            ],
            axis=dim,
        )
    return cells


def cross_rows(left, right):
    return lax.dot_general(
        left,
        right,
        (((1,), (1,)), ((), ())),
        precision=lax.Precision.HIGHEST,
        preferred_element_type=jnp.float32,
    )


def held_value(field, spot):
    return jnp.take_along_axis(field, spot, axis=1)


def shards(signal, valid_start, valid_end):
    rows, width = signal.shape
    taps = 2 * HALF + 1
    offsets = jnp.arange(-HALF, HALF + 1).astype(jnp.float32)
    second = jnp.sum(offsets * offsets)
    centre_sq = second / taps
    curved = offsets * offsets - centre_sq
    fourth = jnp.sum(curved * curved)
    extended = padded(signal, (("tm", 1),), 2 * HALF)
    span = width + 2 * HALF
    level = jnp.zeros((rows, span), jnp.float32)
    tilt = jnp.zeros((rows, span), jnp.float32)
    bend = jnp.zeros((rows, span), jnp.float32)
    for m in range(taps):
        window = extended[:, m : m + span]
        level = level + window * (1.0 / taps)
        tilt = tilt + window * (offsets[m] / second)
        bend = bend + window * (curved[m] / fourth)
    begin = lax.axis_index("tm") * width
    group = lax.axis_index("series") * rows
    first = lax.dynamic_slice_in_dim(valid_start, group, rows)[:, None]
    last = lax.dynamic_slice_in_dim(valid_end, group, rows)[:, None]
    moment = begin + jnp.arange(width, dtype=jnp.int32)[None, :]
    low_centre = first + HALF
    high_centre = last - HALF - 1
    centre = jnp.clip(moment, low_centre, high_centre)
    low_spot = jnp.clip(low_centre - begin + HALF, 0, span - 1)
    high_spot = jnp.clip(high_centre - begin + HALF, 0, span - 1)
    below = moment < low_centre
    above = moment > high_centre
    along = (moment - centre).astype(jnp.float32)
    lv = jnp.where(
        below,
        held_value(level, low_spot),
        jnp.where(above, held_value(level, high_spot), level[:, HALF : HALF + width]),
    )
    tl = jnp.where(
        below,
        held_value(tilt, low_spot),
        jnp.where(above, held_value(tilt, high_spot), tilt[:, HALF : HALF + width]),
    )
    bd = jnp.where(
        below,
        held_value(bend, low_spot),
        jnp.where(above, held_value(bend, high_spot), bend[:, HALF : HALF + width]),
    )
    inside = (moment >= first) & (moment < last)
    smooth = jnp.where(inside, lv + tl * along + bd * (along * along - centre_sq), 0.0)
    slope = jnp.where(inside, HALF * (tl + 2.0 * along * bd), 0.0)
    resid = jnp.where(inside, signal - smooth, 0.0)
    mixed = lax.all_to_all(resid, "series", split_axis=1, concat_axis=0, tiled=True)
    full = lax.psum(cross_rows(mixed, mixed), ("tm", "series"))
    gram = lax.dynamic_slice_in_dim(full, group, rows)
    correlation = (
        jnp.minimum(last, valid_end[None, :]) - jnp.maximum(first, valid_start[None, :])
    ).astype(jnp.float32)
    return (smooth, slope, gram / correlation)


def solution(mesh):
    in_specs = (P("series", "tm"), P(), P())
    out_specs = (P("series", "tm"), P("series", "tm"), P("series", None))
    return jax.shard_map(shards, mesh=mesh, in_specs=in_specs, out_specs=out_specs, check_vma=False)
```

profile of v0, /device:TPU:0, one launch (start us, length us, event | category | flops | bytes accessed | tf_op | source)
XLA Modules:
  0.0 258.8 jit_solution(5672851760717426179)
XLA Ops:
  0.6 0.8 fusion.14
  1.4 4.9 %collective-permute-start = (f32[16,32]{1,0:T(8,128)S(1)}, f32[16,32]{1,0:T(8,128)S(1)}, u32[]{:S(2)}, u32[]{:S(2)}) collective-permute-start(f32[16,32]{1,0:T(8,128)S(1)} %get-tuple-element.11), channel_id=1, source_target_pairs={{0,4},{4,8},{8,12},{12,16},{16,20},{20,24},{24,28},{1,5},{5,9},{9,... | collective-permute-start | bytes 6152 | tf_op jit(solution)/shard_map/ppermute | solution.py:17
  6.3 1.3 collective-permute-start.1
  7.6 0.6 multiply_reduce_fusion.1
  8.9 0.7 multiply_reduce_fusion
  9.6 0.7 fusion.18
  10.3 0.7 fusion.17
  11.0 0.7 fusion.16
  11.7 0.7 fusion.15
  12.4 0.0 copy-start.1
  12.4 3.1 %constant_dynamic-update-slice_fusion.1 = f32[16,32800]{1,0:T(8,128)} fusion(f32[16,32768]{1,0:T(8,128)} %param.5), kind=kLoop, calls=%fused_computation.27 | loop fusion | bytes 4194304
  15.5 0.1 broadcast_add_fusion.1
  15.6 0.1 broadcast_add_fusion
  103.3 0.3 dynamic-update-slice.2
  103.6 6.4 %dynamic-update-slice.3 = f32[16,32832]{1,0:T(8,128)S(1)} dynamic-update-slice(f32[16,32832]{1,0:T(8,128)S(1)} %dynamic-update-slice.2, f32[16,32768]{1,0:T(8,128)} %param.5, s32[]{} %constant.163, s32[]{} %constant.165) | dynamic-update-slice | bytes 4194308
  109.9 0.6 constant_dynamic-update-slice_fusion
  110.5 0.2 dynamic-update-slice.4
  110.7 19.9 %multiply_add_fusion.1 = f32[16,32800]{1,0:T(8,128)} fusion(f32[16,32800]{1,0:T(8,128)} %constant_dynamic-update-slice_fusion, f32[16,32832]{1,0:T(8,128)S(1)} %dynamic-update-slice.4, f32[16,32768]{1,0:T(8,128)} %param.5, f32[16,32]{1,0:T(8,128)S(1)} %collective-permute-done, f32[]{:T(128)S(6)} %div.236, f32[]{:T(128)S(6)} %div.235, f32[]{:T(128)S(6)} %div.234, ...), kind=kLoop, calls=%fused_computation.15 | loop fusion | flops 34636800 | bytes 71372928 | tf_op jit(solution)/shard_map/add | solution.py:56
  130.6 1.6 gather_fusion.3
  132.2 1.5 gather_fusion.2
  133.7 20.0 %add_multiply_fusion = f32[16,32800]{1,0:T(8,128)} fusion(f32[16,32800]{1,0:T(8,128)} %constant_dynamic-update-slice_fusion, f32[16,32832]{1,0:T(8,128)S(1)} %dynamic-update-slice.4, f32[16,32768]{1,0:T(8,128)} %param.5, f32[16,32]{1,0:T(8,128)S(1)} %collective-permute-done), kind=kLoop, calls=%fused_computation.13 | loop fusion | flops 17843200 | bytes 71372800 | tf_op jit(solution)/shard_map/add | solution.py:55
  153.8 1.6 gather_fusion.1
  155.4 1.5 gather_fusion
  156.9 19.9 %multiply_add_fusion = f32[16,32800]{1,0:T(8,128)} fusion(f32[16,32800]{1,0:T(8,128)} %constant_dynamic-update-slice_fusion, f32[16,32832]{1,0:T(8,128)S(1)} %dynamic-update-slice.4, f32[16,32768]{1,0:T(8,128)} %param.5, f32[16,32]{1,0:T(8,128)S(1)} %collective-permute-done, f32[]{:T(128)S(6)} %div.270, f32[]{:T(128)S(6)} %div.269, f32[]{:T(128)S(6)} %div.268, ...), kind=kLoop, calls=%fused_computation.14 | loop fusion | flops 34636800 | bytes 71372928 | tf_op jit(solution)/shard_map/add | solution.py:57
  176.8 1.6 gather_fusion.5
  178.4 1.5 gather_fusion.4
  180.0 6.0 %subtract_select_fusion = (f32[16,32768]{1,0:T(8,128)S(1)}, f32[16,32768]{1,0:T(8,128)}, f32[16,32768]{1,0:T(8,128)}) fusion(f32[16,32768]{1,0:T(8,128)} %param.5, s32[32768]{0:T(1024)S(1)} %iota_add_fusion, s32[16]{0:T(128)S(1)} %get-tuple-element.9, s32[16]{0:T(128)S(1)} %get-tuple-element.7, f32[]{:T(128)S(6)} %div.237, f32[16,32800]{1,0:T(8,128)} %multiply_add_fusion, ...), kind=kLoop, calls=%fused_computation.20 | loop fusion | flops 15204352 | bytes 14811780 | tf_op jit(solution)/shard_map/jit(_where)/select_n | solution.py:89
  186.0 0.1 copy.9
  186.1 28.3 %all_to_all.19 = f32[16,4,8192]{2,0,1:T(8,128)S(1)} all-to-all(f32[16,4,8192]{2,0,1:T(8,128)S(1)} %bitcast.161), channel_id=1, replica_groups=mesh['tm'=8,'series'=4] {'series'}, dimensions={1} | all-to-all | bytes 4194304 | tf_op jit(solution)/shard_map/all_to_all | solution.py:90
  214.5 1.8 fusion.19
  216.2 41.9 %psum.7 = f32[64,64]{1,0:T(8,128)S(1)} all-reduce(f32[64,64]{1,0:T(8,128)S(1)} %fusion.19), channel_id=1, replica_groups=mesh['tm'=8,'series'=4] {'tm','series'}, use_global_device_ids=true, to_apply=%region_2.4 | all-reduce | flops 4096 | bytes 32768 | tf_op jit(solution)/shard_map/psum | solution.py:91
  258.1 0.7 convert_divide_fusion
  (16 shorter events, 0.1 us)
Async XLA Ops:
  1.4 101.8 %collective-permute-start = (f32[16,32]{1,0:T(8,128)S(1)}, f32[16,32]{1,0:T(8,128)S(1)}, u32[]{:S(2)}, u32[]{:S(2)}) collective-permute-start(f32[16,32]{1,0:T(8,128)S(1)} %get-tuple-element.11), channel_id=1, source_target_pairs={{0,4},{4,8},{8,12},{12,16},{16,20},{20,24},{24,28},{1,5},{5,9},{9,... | collective-permute-start | bytes 6152 | tf_op jit(solution)/shard_map/ppermute | solution.py:17
  6.3 103.6 %collective-permute-start.1 = (f32[16,32]{1,0:T(8,128)S(1)}, f32[16,32]{1,0:T(8,128)S(1)}, u32[]{:S(2)}, u32[]{:S(2)}) collective-permute-start(f32[16,32]{1,0:T(8,128)S(1)} %get-tuple-element.12), channel_id=1, source_target_pairs={{4,0},{8,4},{12,8},{16,12},{20,16},{24,20},{28,24},{5,1},{9,5},{13... | collective-permute-start | bytes 6152 | tf_op jit(solution)/shard_map/ppermute | solution.py:19
  12.4 3.1 %copy-start.1 = (s32[64]{0:T(128)S(1)}, s32[64]{0:T(128)}, u32[]{:S(2)}) copy-start(s32[64]{0:T(128)} %param.6) | copy-start | bytes 772
  12.4 3.2 %copy-start = (s32[64]{0:T(128)S(1)}, s32[64]{0:T(128)}, u32[]{:S(2)}) copy-start(s32[64]{0:T(128)} %param.7) | copy-start | bytes 772
where the time goes:
time: 261 us; the launch traced here: 259 us
  between operations  88.9 us (34%)
  blocking collectives  70.2 us (27%)
  other arithmetic  68 us (26%)
  local copies, waits for them, and re-layouts  23.7 us (9%)
  starting transfers between devices  6.18 us (2%)
    psum x1, blocking collectives, shards(): full = lax.psum(cross_rows(mixed, mixed), ('tm', 'series'))  41.9 us
    all_to_all x1, blocking collectives, shards(): lax.all_to_all(resid, 'series', split_axis=1, concat_axis=0, tiled=True)  28.3 us
    add x1, other arithmetic, shards(): level = level + window * (1.0 / taps)  20 us
    add x1, other arithmetic, shards(): tilt = tilt + window * (offsets[m] / second)  19.9 us
    add x1, other arithmetic, shards(): bend = bend + window * (curved[m] / fourth)  19.9 us
    unnamed x7, local copies, waits for them, and re-layouts  9.73 us
    gather x6, local copies, waits for them, and re-layouts, held_value(): return jnp.take_along_axis(field, spot, axis=1)  9.45 us
    select_n x1, other arithmetic, shards(): resid = jnp.where(inside, signal - smooth, 0.0)  5.98 us
  transfers between devices with their start and end apart: 2, of which 0 were waited for; matrix products, arithmetic and copies ran while one was open for 5% of the time, Pallas kernels for 0%

commit v1 on v0

--- a/solution.py
+++ b/solution.py
@@ -87,7 +87,10 @@
     smooth = jnp.where(inside, lv + tl * along + bd * (along * along - centre_sq), 0.0)
     slope = jnp.where(inside, HALF * (tl + 2.0 * along * bd), 0.0)
     resid = jnp.where(inside, signal - smooth, 0.0)
-    mixed = lax.all_to_all(resid, "series", split_axis=1, concat_axis=0, tiled=True)
+    peers = lax.axis_size("series")
+    pieces = jnp.stack(jnp.split(resid, peers, axis=1), axis=0)
+    pieces = lax.all_to_all(pieces, "series", split_axis=0, concat_axis=0)
+    mixed = jnp.concatenate(pieces, axis=0)
     full = lax.psum(cross_rows(mixed, mixed), ("tm", "series"))
     gram = lax.dynamic_slice_in_dim(full, group, rows)
     correlation = (

time: 261 us -> 261 us (level)
  no operation moved by 1% of the time
where the time goes in v1:
time: 261 us; the launch traced here: 259 us
  between operations  88.8 us (34%)
  blocking collectives  70.2 us (27%)
  other arithmetic  68.1 us (26%)
  local copies, waits for them, and re-layouts  23.8 us (9%)
  starting transfers between devices  6.18 us (2%)
    psum x1, blocking collectives, shards(): full = lax.psum(cross_rows(mixed, mixed), ('tm', 'series'))  41.9 us
    all_to_all x1, blocking collectives, shards(): pieces = lax.all_to_all(pieces, 'series', split_axis=0, concat_axis=0)  28.4 us
    add x1, other arithmetic, shards(): level = level + window * (1.0 / taps)  20 us
    add x1, other arithmetic, shards(): tilt = tilt + window * (offsets[m] / second)  19.9 us
    add x1, other arithmetic, shards(): bend = bend + window * (curved[m] / fourth)  19.9 us
    unnamed x7, local copies, waits for them, and re-layouts  9.75 us
    gather x6, local copies, waits for them, and re-layouts, held_value(): return jnp.take_along_axis(field, spot, axis=1)  9.46 us
    select_n x1, other arithmetic, shards(): resid = jnp.where(inside, signal - smooth, 0.0)  5.98 us
  transfers between devices with their start and end apart: 2, of which 0 were waited for; matrix products, arithmetic and copies ran while one was open for 5% of the time, Pallas kernels for 0%

profile of v1, /device:TPU:0, one launch (start us, length us, event | category | flops | bytes accessed | tf_op | source)
XLA Modules:
  0.0 258.9 jit_solution(16074832601618632375)
XLA Ops:
  0.6 0.8 fusion.14
  1.4 4.9 %collective-permute-start = (f32[16,32]{1,0:T(8,128)S(1)}, f32[16,32]{1,0:T(8,128)S(1)}, u32[]{:S(2)}, u32[]{:S(2)}) collective-permute-start(f32[16,32]{1,0:T(8,128)S(1)} %get-tuple-element.15), channel_id=1, source_target_pairs={{0,4},{4,8},{8,12},{12,16},{16,20},{20,24},{24,28},{1,5},{5,9},{9,... | collective-permute-start | bytes 6152 | tf_op jit(solution)/shard_map/ppermute | solution.py:17
  6.3 1.3 collective-permute-start.1
  7.6 0.6 multiply_reduce_fusion.1
  8.9 0.7 multiply_reduce_fusion
  9.6 0.7 fusion.18
  10.3 0.7 fusion.17
  11.0 0.7 fusion.16
  11.7 0.7 fusion.15
  12.4 3.1 %constant_dynamic-update-slice_fusion.1 = f32[16,32800]{1,0:T(8,128)} fusion(f32[16,32768]{1,0:T(8,128)} %param.5), kind=kLoop, calls=%fused_computation.31 | loop fusion | bytes 4194304
  15.6 0.1 broadcast_add_fusion.1
  15.7 0.1 broadcast_add_fusion
  103.2 0.3 dynamic-update-slice.2
  103.5 6.4 %dynamic-update-slice.3 = f32[16,32832]{1,0:T(8,128)S(1)} dynamic-update-slice(f32[16,32832]{1,0:T(8,128)S(1)} %dynamic-update-slice.2, f32[16,32768]{1,0:T(8,128)} %param.5, s32[]{} %constant.164, s32[]{} %constant.166) | dynamic-update-slice | bytes 4194308
  109.9 0.6 constant_dynamic-update-slice_fusion
  110.5 0.2 dynamic-update-slice.4
  110.6 19.9 %multiply_add_fusion.1 = f32[16,32800]{1,0:T(8,128)} fusion(f32[16,32800]{1,0:T(8,128)} %constant_dynamic-update-slice_fusion, f32[16,32832]{1,0:T(8,128)S(1)} %dynamic-update-slice.4, f32[16,32768]{1,0:T(8,128)} %param.5, f32[16,32]{1,0:T(8,128)S(1)} %collective-permute-done, f32[]{:T(128)S(6)} %div.236, f32[]{:T(128)S(6)} %div.235, f32[]{:T(128)S(6)} %div.234, ...), kind=kLoop, calls=%fused_computation.15 | loop fusion | flops 34636800 | bytes 71372928 | tf_op jit(solution)/shard_map/add | solution.py:56
  130.5 1.6 gather_fusion.3
  132.2 1.5 gather_fusion.2
  133.7 20.0 %add_multiply_fusion = f32[16,32800]{1,0:T(8,128)} fusion(f32[16,32800]{1,0:T(8,128)} %constant_dynamic-update-slice_fusion, f32[16,32832]{1,0:T(8,128)S(1)} %dynamic-update-slice.4, f32[16,32768]{1,0:T(8,128)} %param.5, f32[16,32]{1,0:T(8,128)S(1)} %collective-permute-done), kind=kLoop, calls=%fused_computation.13 | loop fusion | flops 17843200 | bytes 71372800 | tf_op jit(solution)/shard_map/add | solution.py:55
  153.7 1.6 gather_fusion.1
  155.3 1.5 gather_fusion
  156.9 19.9 %multiply_add_fusion = f32[16,32800]{1,0:T(8,128)} fusion(f32[16,32800]{1,0:T(8,128)} %constant_dynamic-update-slice_fusion, f32[16,32832]{1,0:T(8,128)S(1)} %dynamic-update-slice.4, f32[16,32768]{1,0:T(8,128)} %param.5, f32[16,32]{1,0:T(8,128)S(1)} %collective-permute-done, f32[]{:T(128)S(6)} %div.270, f32[]{:T(128)S(6)} %div.269, f32[]{:T(128)S(6)} %div.268, ...), kind=kLoop, calls=%fused_computation.14 | loop fusion | flops 34636800 | bytes 71372928 | tf_op jit(solution)/shard_map/add | solution.py:57
  176.7 1.6 gather_fusion.5
  178.4 1.5 gather_fusion.4
  179.9 6.0 %subtract_select_fusion = (f32[16,32768]{1,0:T(8,128)S(1)}, f32[16,32768]{1,0:T(8,128)}, f32[16,32768]{1,0:T(8,128)}) fusion(f32[16,32768]{1,0:T(8,128)} %param.5, s32[32768]{0:T(1024)S(1)} %iota_add_fusion, s32[16]{0:T(128)S(1)} %get-tuple-element.9, s32[16]{0:T(128)S(1)} %get-tuple-element.7, f32[]{:T(128)S(6)} %div.237, f32[16,32800]{1,0:T(8,128)} %multiply_add_fusion, ...), kind=kLoop, calls=%fused_computation.20 | loop fusion | flops 15204352 | bytes 14811780 | tf_op jit(solution)/shard_map/jit(_where)/select_n | solution.py:89
  185.9 0.1 slice_bitcast_fusion.3
  186.0 0.1 pad_maximum_fusion.1
  186.2 28.4 %all_to_all.5 = f32[4,16,8192]{2,1,0:T(8,128)S(1)} all-to-all(f32[4,16,8192]{2,1,0:T(8,128)S(1)} %pad_maximum_fusion.1), channel_id=1, replica_groups=mesh['tm'=8,'series'=4] {'series'}, dimensions={0} | all-to-all | bytes 4194304 | tf_op jit(solution)/shard_map/all_to_all | solution.py:92
  214.5 1.8 fusion.19
  216.3 41.9 %psum.7 = f32[64,64]{1,0:T(8,128)S(1)} all-reduce(f32[64,64]{1,0:T(8,128)S(1)} %fusion.19), channel_id=1, replica_groups=mesh['tm'=8,'series'=4] {'tm','series'}, use_global_device_ids=true, to_apply=%region_2.4 | all-reduce | flops 4096 | bytes 32768 | tf_op jit(solution)/shard_map/psum | solution.py:94
  258.2 0.7 convert_divide_fusion
  (17 shorter events, 0.1 us)
Async XLA Ops:
  1.4 101.8 %collective-permute-start = (f32[16,32]{1,0:T(8,128)S(1)}, f32[16,32]{1,0:T(8,128)S(1)}, u32[]{:S(2)}, u32[]{:S(2)}) collective-permute-start(f32[16,32]{1,0:T(8,128)S(1)} %get-tuple-element.15), channel_id=1, source_target_pairs={{0,4},{4,8},{8,12},{12,16},{16,20},{20,24},{24,28},{1,5},{5,9},{9,... | collective-permute-start | bytes 6152 | tf_op jit(solution)/shard_map/ppermute | solution.py:17
  6.3 103.5 %collective-permute-start.1 = (f32[16,32]{1,0:T(8,128)S(1)}, f32[16,32]{1,0:T(8,128)S(1)}, u32[]{:S(2)}, u32[]{:S(2)}) collective-permute-start(f32[16,32]{1,0:T(8,128)S(1)} %get-tuple-element.16), channel_id=1, source_target_pairs={{4,0},{8,4},{12,8},{16,12},{20,16},{24,20},{28,24},{5,1},{9,5},{13... | collective-permute-start | bytes 6152 | tf_op jit(solution)/shard_map/ppermute | solution.py:19
  12.4 3.1 %copy-start.1 = (s32[64]{0:T(128)S(1)}, s32[64]{0:T(128)}, u32[]{:S(2)}) copy-start(s32[64]{0:T(128)} %param.6) | copy-start | bytes 772
  12.4 3.2 %copy-start = (s32[64]{0:T(128)S(1)}, s32[64]{0:T(128)}, u32[]{:S(2)}) copy-start(s32[64]{0:T(128)} %param.7) | copy-start | bytes 772
